TPU v7x, 256 devices: a whole 4x4x8 slice. The times are simulated.
256 devices in a mesh: band: 32 (over z, y_hi, core), chan: 8 (over x, y_lo).
Axes of the slice: x: 4, y: 4 (y_hi: 2, y_lo: 2; y = y_hi * 2 + y_lo), z: 8, core: 2. Of those that a mesh axis runs over, the one named last changes fastest.
Arguments:
- fine_features: bfloat16 [2, 192, 256, 512], P(None, 'chan', 'band'), may hold values from -100 to 100
- coarse_level: bfloat16 [2, 256, 128, 256], P(None, 'chan', 'band'), may hold values from -100 to 100
- lat_weight: bfloat16 [256, 192], P('chan'), may hold values from -0.4375 to 0.4375
- lat_gain: bfloat16 [256], P('chan'), may hold values from 0.099609375 to 1.8984375
- lat_shift: bfloat16 [256], P('chan'), may hold values from -3 to 3
- out_weight: bfloat16 [3, 3, 256, 256], P(None, None, 'chan'), may hold values from -0.125 to 0.125
- out_gain: bfloat16 [256], P('chan'), may hold values from 0.099609375 to 1.8984375
- out_shift: bfloat16 [256], P('chan'), may hold values from -3 to 3
- mask_weight: bfloat16 [256, 256], P('chan'), may hold values from -0.375 to 0.375
- mask_bias: bfloat16 [256], P('chan'), may hold values from -1.796875 to 1.796875
- queries: bfloat16 [200, 256], replicated, may hold values from -128 to 128
Outputs:
- log_probs: float32 [2, 200, 256, 512], P(None, None, ('band', 'chan'))
All inputs are finite; a program needn't handle non-finite values.
Results may differ from a plain program's by a relative error of at most 0.0058.
Values may be sent and summed in bfloat16 or wider, within the bound.
No kernel may reach another device: no remote copies, remote signals or barrier semaphores. Data moves between devices by JAX's collectives and lax.ppermute only.
A program may use at most 64 MiB of HBM per device.

v0:
```python
import functools

import jax
import jax.numpy as jnp
from jax import lax
from jax.sharding import Mesh
from jax.sharding import PartitionSpec as P

D = 256
GROUPS = 32
BAND = ("band_0", "band_1", "band_2")
CHAN = ("chan_0", "chan_1")
BAND_CHAN = ("band_0", "band_1", "band_2", "chan_0", "chan_1")


epsilon = 1e-05


def whole_of(shard, axes, dim):
    for axis in reversed(axes):
        shard = lax.all_gather(shard, axis, axis=dim, tiled=True)
    return shard


def from_everyone(shard, axis):
    devices = lax.axis_size(axis)
    return lax.all_to_all(
        jnp.broadcast_to(shard[None], (devices, *shard.shape)), axis, 0, 0, tiled=True
    )


def of_everyone(shard, axis):
    everything = from_everyone(shard, axis)
    return jnp.sum(everything, axis=0)


def together(arrays, axis):
    vector, at, done = (jnp.concatenate([a.reshape(-1) for a in arrays]), 0, [])
    total = of_everyone(vector, axis)
    for a in arrays:
        done.append(total[at : at + a.size].reshape(a.shape))
        at += a.size
    return tuple(done)


def extended_2(cells, sides, width):
    for axis, dim in sides:
        count = lax.axis_size(axis)
        ends = count - 1
        head = lax.slice_in_dim(cells, 0, width, axis=dim)
        tail = lax.slice_in_dim(cells, cells.shape[dim] - width, cells.shape[dim], axis=dim)
        cells = jnp.concatenate(
            [
                lax.ppermute(tail, axis, [(i, (i + 1) % count) for i in range(ends)]),
                cells,
                lax.ppermute(head, axis, [((i + 1) % count, i) for i in range(ends)]),
            ],
            axis=dim,
        )
    return cells


def rows_first(arrays, axis, dims):
    turned = [jnp.moveaxis(a, dim, 0) for a, dim in zip(arrays, dims)]
    both = jnp.concatenate([t.reshape(len(t), -1) for t in turned], axis=1)
    result, at, done = (lax.all_gather(both, axis, axis=0, tiled=True), 0, [])
    for t, dim in zip(turned, dims):
        slab = result[:, at : at + t[0].size].reshape(-1, *t.shape[1:])
        done.append(jnp.moveaxis(slab, 0, dim))
        at += t[0].size
    return tuple(done)


def extended_3(shard, sides, width):
    edges = {}
    for axis, dim in sides:
        devices, length = (lax.axis_size(axis), shard.shape[dim])
        up = [(i, (i + 1) % devices) for i in range(devices - 1)]
        last = lax.slice_in_dim(shard, length - width, length, axis=dim)
        first = lax.slice_in_dim(shard, 0, width, axis=dim)
        edges[dim] = (
            lax.ppermute(last, axis, up),
            lax.ppermute(first, axis, [(b, a) for a, b in up]),
        )
    done = []
    for _, dim in sides:
        low, high = edges[dim]
        around = [(width, width) if d in done else (0, 0) for d in range(shard.ndim)]
        shard = jnp.concatenate([jnp.pad(low, around), shard, jnp.pad(high, around)], axis=dim)
        done.append(dim)
    return shard


def over_axes_2(shard, axes):
    return functools.reduce(lax.psum, axes, shard)


def interp(padded, axis):
    length = padded.shape[axis] - 2
    before = lax.slice_in_dim(padded, 0, length, axis=axis)
    middle = lax.slice_in_dim(padded, 1, length + 1, axis=axis)
    after = lax.slice_in_dim(padded, 2, length + 2, axis=axis)
    even_part = 0.25 * before + 0.75 * middle
    odd_part = 0.75 * middle + 0.25 * after
    paired = jnp.stack([even_part, odd_part], axis + 1)
    new_shape = list(middle.shape)
    new_shape[axis] = 2 * length
    return paired.reshape(new_shape)


def conv_taps(taps_weight, padded, row_count, col_count):
    summed = None
    for row_tap in range(3):
        for col_tap in range(3):
            window = padded[:, :, row_tap : row_tap + row_count, col_tap : col_tap + col_count]
            term = jnp.einsum(
                "oc,ncrw->norw",
                taps_weight[row_tap, col_tap],
                window,
                preferred_element_type=jnp.float32,
            )
            summed = term if summed is None else summed + term
    return summed


def apply_norm(blocks, mean_value, variance, full_shape, gain, shift):
    scaled = (
        (blocks - mean_value[:, :, None]) * lax.rsqrt(variance[:, :, None] + epsilon)
    ).reshape(full_shape)
    return (
        scaled * gain.astype(jnp.float32)[None, :, None, None]
        + shift.astype(jnp.float32)[None, :, None, None]
    )


def per_device(
    fine_features,
    coarse_level,
    lat_weight,
    lat_gain,
    lat_shift,
    out_weight,
    out_gain,
    out_shift,
    mask_weight,
    mask_bias,
    queries,
):
    images, in_share, band_rows, columns = fine_features.shape
    out_share = lat_weight.shape[0]
    group_size = D // GROUPS
    band_count = lax.axis_size(BAND)
    pixel_count = float(group_size * band_rows * band_count * columns)
    lateral = jnp.einsum(
        "oc,ncrw->norw",
        lat_weight,
        whole_of(fine_features, CHAN, 1),
        preferred_element_type=jnp.float32,
    )
    lat_blocks = lateral.reshape(images, out_share // group_size, -1)
    first_sum, square_sum = together(
        (jnp.sum(lat_blocks, 2), jnp.sum(lat_blocks * lat_blocks, 2)), BAND
    )
    lat_mean = first_sum / pixel_count
    lat_var = square_sum / pixel_count - lat_mean * lat_mean
    lat_normed = apply_norm(lat_blocks, lat_mean, lat_var, lateral.shape, lat_gain, lat_shift)
    band_index = lax.axis_index(BAND)
    extended = extended_2(coarse_level, ((BAND, 2),), 1)
    top_row = jnp.where(band_index == 0, extended[:, :, 1:2], extended[:, :, 0:1])
    bottom_row = jnp.where(band_index == band_count - 1, extended[:, :, -2:-1], extended[:, :, -1:])
    extended = jnp.concatenate([top_row, extended[:, :, 1:-1], bottom_row], 2).astype(jnp.float32)
    extended = jnp.pad(extended, ((0, 0), (0, 0), (0, 0), (1, 1)), mode="edge")
    upsampled = interp(interp(extended, 2), 3)
    joined = (lat_normed + upsampled).astype(jnp.bfloat16)
    row_joined = lax.all_to_all(joined, CHAN, split_axis=2, concat_axis=1, tiled=True)
    conv_weight, full_gain, full_shift, full_mask, full_bias = rows_first(
        (out_weight, out_gain, out_shift, mask_weight, mask_bias), CHAN, (2, 0, 0, 0, 0)
    )
    row_count = row_joined.shape[2]
    padded = extended_3(row_joined, ((BAND_CHAN, 2),), 1)
    padded = jnp.pad(padded, ((0, 0), (0, 0), (0, 0), (1, 1)))
    conv_out = conv_taps(conv_weight, padded, row_count, columns)
    local_groups = conv_out.shape[1] // group_size
    conv_blocks = conv_out.reshape(images, local_groups, -1)
    first_sum, square_sum = (
        over_axes_2(jnp.sum(conv_blocks, 2), BAND_CHAN),
        over_axes_2(jnp.sum(conv_blocks * conv_blocks, 2), BAND_CHAN),
    )
    out_mean = first_sum / pixel_count
    out_var = square_sum / pixel_count - out_mean * out_mean
    activated = jnp.maximum(
        apply_norm(conv_blocks, out_mean, out_var, conv_out.shape, full_gain, full_shift), 0.0
    ).astype(jnp.bfloat16)
    mixed = jnp.einsum("oc,ncrw->norw", full_mask, activated, preferred_element_type=jnp.float32)
    features = (mixed + full_bias.astype(jnp.float32)[None, :, None, None]).astype(jnp.bfloat16)
    logits = jnp.einsum("qc,ncrw->nqrw", queries, features, preferred_element_type=jnp.float32)
    peak = jnp.max(logits, axis=1, keepdims=True)
    shifted = logits - peak
    return shifted - jnp.log(jnp.sum(jnp.exp(shifted), axis=1, keepdims=True))


def solution(mesh):
    finer = Mesh(
        mesh.devices.reshape(8, 2, 2, 4, 2), ("band_0", "band_1", "band_2", "chan_0", "chan_1")
    )
    return jax.shard_map(
        per_device,
        mesh=finer,
        in_specs=(
            P(None, CHAN, BAND, None),
            P(None, CHAN, BAND, None),
            P(CHAN, None),
            P(CHAN),
            P(CHAN),
            P(None, None, CHAN, None),
            P(CHAN),
            P(CHAN),
            P(CHAN, None),
            P(CHAN),
            P(),
        ),
        out_specs=P(None, None, BAND_CHAN, None),
        check_vma=False,
    )
```

profile of v0, /device:TPU:1, one launch (start us, length us, event | category | flops | bytes accessed | tf_op | source)
XLA Modules:
  0.0 194.1 jit_solution(14821775544528148993)
XLA Ops:
  6.6 1.3 copy.111
  7.9 10.6 %all_gather.9 = bf16[2,48,8,512]{3,1,2,0:T(8,128)(2,1)} all-gather(bf16[2,24,8,512]{3,1,2,0:T(8,128)(2,1)S(1)} %copy.111), channel_id=1, replica_groups=mesh['band_0'=8,'band_1'=2,'band_2'=2,'chan_0'=4,'chan_1'=2] {'chan_1'}, dimensions={1}, use_global_device_ids=true | all-gather | bytes 1179648 | tf_op jit(solution)/shard_map/all_gather | solution.py:21
  18.6 7.4 %collective-permute-start = (bf16[2,32,1,256]{3,1,2,0:T(8,128)(2,1)S(1)}, bf16[2,32,1,256]{3,1,2,0:T(8,128)(2,1)S(1)}, u32[]{:S(2)}, u32[]{:S(2)}) collective-permute-start(bf16[2,32,1,256]{3,1,2,0:T(8,128)(2,1)S(1)} %get-tuple-element.30), channel_id=1, source_target_pairs={{0,8},{8,16},{16,24},{24,32},{32,40},{40,48},{48,56},{56,64},{64,7... | collective-permute-start | bytes 98312 | tf_op jit(solution)/shard_map/ppermute | solution.py:54
  26.0 1.9 collective-permute-start.1
  28.2 0.1 copy.126
  28.4 0.2 reshape.197
  28.6 0.8 concatenate.20
  29.4 3.3 %collective-permute-done.1 = bf16[2,32,1,256]{3,1,2,0:T(8,128)(2,1)S(1)} collective-permute-done((bf16[2,32,1,256]{3,1,2,0:T(8,128)(2,1)S(1)}, bf16[2,32,1,256]{3,1,2,0:T(8,128)(2,1)S(1)}, u32[]{:S(2)}, u32[]{:S(2)}) %collective-permute-start.1) | collective-permute-done | bytes 32800 | tf_op jit(solution)/shard_map/ppermute | solution.py:56
  32.8 0.1 fusion.51
  32.9 0.3 pad_maximum_fusion.2
  33.4 0.3 fusion.24
  33.7 31.8 %all-gather.3.cloned.1.call-done = bf16[2,192,8,512]{3,1,2,0:T(8,128)(2,1)} async-done(((bf16[2,48,8,512]{3,1,2,0:T(8,128)(2,1)}), bf16[2,192,8,512]{3,1,2,0:T(8,128)(2,1)}) %all-gather.3.cloned.1.call-update) | async-done | bytes 3145744 | tf_op jit(solution)/shard_map/all_gather | solution.py:21
  65.5 2.7 %fusion.50 = (f32[2,32]{1,0:T(2,128)S(1)}, f32[2,32]{1,0:T(2,128)S(1)}, f32[2,32,8,512]{3,1,2,0:T(8,128)S(1)}) fusion(bf16[2,192,8,512]{3,1,2,0:T(8,128)(2,1)} %all-gather.3.cloned.1.call-done, bf16[32,192]{1,0:T(8,128)(2,1)S(1)} %copy-done.5), kind=kOutput, calls=%fused_computation.91 | convolution fusion | flops 101449600 | bytes 4207104 | tf_op jit(solution)/shard_map/oc,ncrw->norw/dot_general | solution.py:154
  68.7 0.6 broadcast_in_dim.2
  69.4 10.5 %all-to-all-start = ((f32[32,1,16]{2,1,0:T(1,128)}), f32[32,1,16]{2,1,0:T(1,128)S(1)}, u32[]{:S(2)}, u32[]{:S(2)}) async-start(f32[32,1,16]{2,1,0:T(1,128)} %broadcast_in_dim.2), calls=%async_computation | async-start | bytes 32768 | tf_op jit(solution)/shard_map/all_to_all | solution.py:27
  79.9 3.7 %copy.119 = f32[2,32,8,256,2]{1,2,4,3,0:T(8,128)} copy(f32[2,32,8,256,2]{3,1,2,0,4:T(8,128)S(1)} %pad_maximum_fusion) | data formatting | bytes 2097152 | tf_op jit(solution)/shard_map/stack | solution.py:105
  83.6 2.8 %copy.120 = f32[2,32,8,512]{3,1,2,0:T(8,128)S(1)} copy(f32[2,32,8,512]{1,2,3,0:T(8,128)} %bitcast.154) | data formatting | bytes 2097152 | tf_op jit(solution)/shard_map/reshape | solution.py:108
  86.4 2.7 %all-to-all-done = f32[32,1,16]{2,1,0:T(1,128)S(1)} async-done(((f32[32,1,16]{2,1,0:T(1,128)}), f32[32,1,16]{2,1,0:T(1,128)S(1)}, u32[]{:S(2)}, u32[]{:S(2)}) %all-to-all-start) | async-done | bytes 2080 | tf_op jit(solution)/shard_map/all_to_all | solution.py:27
  89.8 0.4 add_convert_fusion
  90.2 14.5 %all_to_all.24 = bf16[2,32,8,512]{3,1,0,2:T(8,128)(2,1)S(1)} all-to-all(bf16[2,32,8,512]{3,1,0,2:T(8,128)(2,1)S(1)} %copy.121), channel_id=1, replica_groups=mesh['band_0'=8,'band_1'=2,'band_2'=2,'chan_0'=4,'chan_1'=2] {'chan_0','..., dimensions={2} | all-to-all | bytes 1048576 | tf_op jit(solution)/shard_map/all_to_all | solution.py:175
  104.7 1.0 copy.123
  105.7 4.7 %collective-permute-start.3 = (bf16[2,256,1,512]{1,3,0,2:T(8,128)(2,1)}, bf16[2,256,1,512]{1,3,0,2:T(8,128)(2,1)}, u32[]{:S(2)}, u32[]{:S(2)}) collective-permute-start(bf16[2,256,1,512]{1,3,0,2:T(8,128)(2,1)} %copy.123), channel_id=1, source_target_pairs={{1,0},{2,1},{3,2},{4,3},{5,4},{6,5},{7,6},{8,7},{9,8},{10,9},{11,1... | collective-permute-start | bytes 1572872 | tf_op jit(solution)/shard_map/ppermute | solution.py:83
  110.5 1.9 collective-permute-start.2
  112.4 12.1 %all-gather.5.cloned.1.call-done = bf16[256,2563]{1,0:T(8,128)(2,1)} async-done(((bf16[32,2563]{1,0:T(8,128)(2,1)}), bf16[256,2563]{1,0:T(8,128)(2,1)}) %all-gather.5.cloned.1.call-update) | async-done | bytes 1312272 | tf_op jit(solution)/shard_map/all_gather | solution.py:66
  124.5 1.3 slice-done
  125.7 0.6 copy.130
  126.3 1.6 copy.131
  127.9 0.2 convert_reduce_fusion.2
  128.1 1.3 fusion.44
  129.4 1.9 collective-permute-done.3
  131.2 4.4 %collective-permute-done.2 = bf16[2,256,1,512]{1,3,0,2:T(8,128)(2,1)} collective-permute-done((bf16[2,256,1,512]{1,3,0,2:T(8,128)(2,1)}, bf16[2,256,1,512]{1,3,0,2:T(8,128)(2,1)}, u32[]{:S(2)}, u32[]{:S(2)}) %collective-permute-start.2) | collective-permute-done | bytes 524320 | tf_op jit(solution)/shard_map/ppermute | solution.py:82
  135.6 1.7 fusion.5
  137.4 0.3 fusion.17
  137.7 0.3 fusion.18
  138.0 0.3 fusion.19
  138.4 0.3 fusion.20
  138.7 0.3 fusion.16
  139.1 1.4 fusion.27
  140.4 1.4 fusion.25
  141.8 1.6 fusion.49
  143.8 14.1 %all-reduce.1 = (f32[2,32]{1,0:T(2,128)S(1)}, f32[2,32]{1,0:T(2,128)S(1)}) all-reduce(f32[2,32]{1,0:T(2,128)S(1)} %reduce_sum.94, f32[2,32]{1,0:T(2,128)S(1)} %reduce_sum.91), channel_id=1, replica_groups=mesh['band_0'=8,'band_1'=2,'band_2'=2,'chan_0'=4,'chan_1'=2] {'band_0'}, use_global_device_ids=true, to_apply=%region_14.15 | all-reduce | flops 128 | bytes 1024 | tf_op jit(solution)/shard_map/psum | solution.py:95
  158.0 5.3 %all-reduce.5 = (f32[2,32]{1,0:T(2,128)S(1)}, f32[2,32]{1,0:T(2,128)S(1)}) all-reduce(f32[2,32]{1,0:T(2,128)S(1)} %get-tuple-element.12, f32[2,32]{1,0:T(2,128)S(1)} %get-tuple-element.13), channel_id=1, replica_groups=mesh['band_0'=8,'band_1'=2,'band_2'=2,'chan_0'=4,'chan_1'=2] {'band_1'}, use_global_device_ids=true, to_apply=%region_15.16 | all-reduce | flops 128 | bytes 1024 | tf_op jit(solution)/shard_map/psum | solution.py:95
  163.2 7.2 %all-reduce.4 = (f32[2,32]{1,0:T(2,128)S(1)}, f32[2,32]{1,0:T(2,128)S(1)}) all-reduce(f32[2,32]{1,0:T(2,128)S(1)} %get-tuple-element.20, f32[2,32]{1,0:T(2,128)S(1)} %get-tuple-element.21), channel_id=1, replica_groups=mesh['band_0'=8,'band_1'=2,'band_2'=2,'chan_0'=4,'chan_1'=2] {'band_2'}, use_global_device_ids=true, to_apply=%region_16.17 | all-reduce | flops 128 | bytes 1024 | tf_op jit(solution)/shard_map/psum | solution.py:95
  170.4 8.8 %all-reduce.2 = (f32[2,32]{1,0:T(2,128)S(1)}, f32[2,32]{1,0:T(2,128)S(1)}) all-reduce(f32[2,32]{1,0:T(2,128)S(1)} %get-tuple-element.18, f32[2,32]{1,0:T(2,128)S(1)} %get-tuple-element.19), channel_id=1, replica_groups=mesh['band_0'=8,'band_1'=2,'band_2'=2,'chan_0'=4,'chan_1'=2] {'chan_0'}, use_global_device_ids=true, to_apply=%region_17.18 | all-reduce | flops 128 | bytes 1024 | tf_op jit(solution)/shard_map/psum | solution.py:95
  179.2 3.8 %all-reduce.3 = (f32[2,32]{1,0:T(2,128)S(1)}, f32[2,32]{1,0:T(2,128)S(1)}) all-reduce(f32[2,32]{1,0:T(2,128)S(1)} %get-tuple-element.14, f32[2,32]{1,0:T(2,128)S(1)} %get-tuple-element.15), channel_id=1, replica_groups=mesh['band_0'=8,'band_1'=2,'band_2'=2,'chan_0'=4,'chan_1'=2] {'chan_1'}, use_global_device_ids=true, to_apply=%region_18.19 | all-reduce | flops 128 | bytes 1024 | tf_op jit(solution)/shard_map/psum | solution.py:95
  183.3 1.9 %fusion.53 = (f32[2,512]{1,0:T(2,128)S(1)}, f32[2,200,1,512]{3,1,0,2:T(8,128)S(1)}) fusion(bf16[200,256]{1,0:T(8,128)(2,1)S(1)} %copy-done, f32[2,256,1,512]{1,3,0,2:T(8,128)} %get-tuple-element.37, f32[256]{0:T(256)S(1)} %get-tuple-element.6, f32[256]{0:T(256)S(1)} %get-tuple-element.7, f32[256]{0:T(256)S(1)} %get-tuple-element.5, f32[2,256]{1,0:T(2,128)S(1)} %mul.108, ...), kind=kOutput, calls=%fused_computation.94 | convolution fusion | flops 241376256 | bytes 2112512 | tf_op jit(solution)/shard_map/qc,ncrw->nqrw/dot_general | solution.py:196
  185.3 0.1 exponential_reduce_fusion
  185.6 1.7 copy.134
  (71 shorter events, 2.9 us)
Async XLA Ops:
  6.5 176.8 %copy-start = (bf16[200,256]{1,0:T(8,128)(2,1)S(1)}, bf16[200,256]{1,0:T(8,128)(2,1)}, u32[]{:S(2)}) copy-start(bf16[200,256]{1,0:T(8,128)(2,1)} %param.21) | copy-start | bytes 307204
  6.5 12.0 %copy-start.4 = (bf16[2,32,4,256]{3,2,1,0:T(4,128)(2,1)S(1)}, bf16[2,32,4,256]{3,2,1,0:T(4,128)(2,1)}, u32[]{:S(2)}) copy-start(bf16[2,32,4,256]{3,2,1,0:T(4,128)(2,1)} %param.12) | copy-start | bytes 393220
  6.5 21.4 %copy-start.7 = (bf16[32]{0:T(256)(128)(2,1)S(1)}, bf16[32]{0:T(256)(128)(2,1)}, u32[]{:S(2)}) copy-start(bf16[32]{0:T(256)(128)(2,1)} %param.17) | copy-start | bytes 196
  6.5 21.5 %copy-start.8 = (bf16[32]{0:T(256)(128)(2,1)S(1)}, bf16[32]{0:T(256)(128)(2,1)}, u32[]{:S(2)}) copy-start(bf16[32]{0:T(256)(128)(2,1)} %param.18) | copy-start | bytes 196
  6.5 21.6 %copy-start.9 = (bf16[32]{0:T(256)(128)(2,1)S(1)}, bf16[32]{0:T(256)(128)(2,1)}, u32[]{:S(2)}) copy-start(bf16[32]{0:T(256)(128)(2,1)} %param.20) | copy-start | bytes 196
  6.5 21.7 %copy-start.3 = (bf16[3,3,32,256]{3,2,1,0:T(8,128)(2,1)S(1)}, bf16[3,3,32,256]{3,2,1,0:T(8,128)(2,1)}, u32[]{:S(2)}) copy-start(bf16[3,3,32,256]{3,2,1,0:T(8,128)(2,1)} %param.16) | copy-start | bytes 442372
  6.6 58.9 %all-gather.3.cloned.1.call-start = ((), (), s32[]{:S(2)}) async-start(), calls=%async_computation.2 | async-start | bytes 3932160 | tf_op jit(solution)/shard_map/all_gather | solution.py:21
  7.9 20.7 %copy-start.6 = (bf16[32,256]{1,0:T(8,128)(2,1)S(1)}, bf16[32,256]{1,0:T(8,128)(2,1)}, u32[]{:S(2)}) copy-start(bf16[32,256]{1,0:T(8,128)(2,1)} %param.19) | copy-start | bytes 49156
  7.9 21.5 %copy-start.10 = (bf16[32]{0:T(256)(128)(2,1)S(1)}, bf16[32]{0:T(256)(128)(2,1)}, u32[]{:S(2)}) copy-start(bf16[32]{0:T(256)(128)(2,1)} %param.14) | copy-start | bytes 196
  7.9 21.5 %copy-start.11 = (bf16[32]{0:T(256)(128)(2,1)S(1)}, bf16[32]{0:T(256)(128)(2,1)}, u32[]{:S(2)}) copy-start(bf16[32]{0:T(256)(128)(2,1)} %param.15) | copy-start | bytes 196
  18.5 105.9 %all-gather.5.cloned.1.call-start = ((), (), s32[]{:S(2)}) async-start(), calls=%async_computation.3 | async-start | bytes 1548288 | tf_op jit(solution)/shard_map/all_gather | solution.py:66
  18.6 10.8 %collective-permute-start = (bf16[2,32,1,256]{3,1,2,0:T(8,128)(2,1)S(1)}, bf16[2,32,1,256]{3,1,2,0:T(8,128)(2,1)S(1)}, u32[]{:S(2)}, u32[]{:S(2)}) collective-permute-start(bf16[2,32,1,256]{3,1,2,0:T(8,128)(2,1)S(1)} %get-tuple-element.30), channel_id=1, source_target_pairs={{0,8},{8,16},{16,24},{24,32},{32,40},{40,48},{48,56},{56,64},{64,7... | collective-permute-start | bytes 98312 | tf_op jit(solution)/shard_map/ppermute | solution.py:54
  26.0 6.7 %collective-permute-start.1 = (bf16[2,32,1,256]{3,1,2,0:T(8,128)(2,1)S(1)}, bf16[2,32,1,256]{3,1,2,0:T(8,128)(2,1)S(1)}, u32[]{:S(2)}, u32[]{:S(2)}) collective-permute-start(bf16[2,32,1,256]{3,1,2,0:T(8,128)(2,1)S(1)} %get-tuple-element.31), channel_id=1, source_target_pairs={{8,0},{16,8},{24,16},{32,24},{40,32},{48,40},{56,48},{64,56},{72,6... | collective-permute-start | bytes 98312 | tf_op jit(solution)/shard_map/ppermute | solution.py:56
  33.3 32.1 %copy-start.5 = (bf16[32,192]{1,0:T(8,128)(2,1)S(1)}, bf16[32,192]{1,0:T(8,128)(2,1)}, u32[]{:S(2)}) copy-start(bf16[32,192]{1,0:T(8,128)(2,1)} %param.13) | copy-start | bytes 36868
  69.4 19.8 %all-to-all-start = ((f32[32,1,16]{2,1,0:T(1,128)}), f32[32,1,16]{2,1,0:T(1,128)S(1)}, u32[]{:S(2)}, u32[]{:S(2)}) async-start(f32[32,1,16]{2,1,0:T(1,128)} %broadcast_in_dim.2), calls=%async_computation | async-start | bytes 32768 | tf_op jit(solution)/shard_map/all_to_all | solution.py:27
  105.7 25.5 %collective-permute-start.3 = (bf16[2,256,1,512]{1,3,0,2:T(8,128)(2,1)}, bf16[2,256,1,512]{1,3,0,2:T(8,128)(2,1)}, u32[]{:S(2)}, u32[]{:S(2)}) collective-permute-start(bf16[2,256,1,512]{1,3,0,2:T(8,128)(2,1)} %copy.123), channel_id=1, source_target_pairs={{1,0},{2,1},{3,2},{4,3},{5,4},{6,5},{7,6},{8,7},{9,8},{10,9},{11,1... | collective-permute-start | bytes 1572872 | tf_op jit(solution)/shard_map/ppermute | solution.py:83
  110.5 25.2 %collective-permute-start.2 = (bf16[2,256,1,512]{1,3,0,2:T(8,128)(2,1)}, bf16[2,256,1,512]{1,3,0,2:T(8,128)(2,1)}, u32[]{:S(2)}, u32[]{:S(2)}) collective-permute-start(bf16[2,256,1,512]{1,3,0,2:T(8,128)(2,1)} %copy.123), channel_id=1, source_target_pairs={{0,1},{1,2},{2,3},{3,4},{4,5},{5,6},{6,7},{7,8},{8,9},{9,10},{10,1... | collective-permute-start | bytes 1572872 | tf_op jit(solution)/shard_map/ppermute | solution.py:82
  124.4 1.3 slice-start
  126.3 1.6 copy-start.1
  129.4 8.0 %copy-start.2 = (bf16[256,3,3,256]{3,0,2,1:T(8,128)(2,1)S(1)}, bf16[256,3,3,256]{3,0,2,1:T(8,128)(2,1)}, u32[]{:S(2)}) copy-start(bf16[256,3,3,256]{3,0,2,1:T(8,128)(2,1)} %copy.131) | copy-start | bytes 3538948
Sparse Core Ops, SparseCore 0:
  18.6 46.7 all-gather.2
  67.3 57.1 all-gather.4
where the time goes:
time: 196 us; the launch traced here: 194 us
  blocking collectives  64.3 us (33%)
  waiting for transfers between devices  56.2 us (29%)
  starting transfers between devices  26.5 us (14%)
  local copies, waits for them, and re-layouts  17.5 us (9%)
  between operations  13.8 us (7%)
  matrix products  11.9 us (6%)
  other arithmetic  4.01 us (2%)
    psum x5, blocking collectives, over_axes_2(): return functools.reduce(lax.psum, axes, shard)  39.2 us
    all_gather x1, waiting for transfers between devices, whole_of(): shard = lax.all_gather(shard, axis, axis=dim, tiled=True)  31.8 us
    all_to_all x1, blocking collectives, per_device(): lax.all_to_all(joined, CHAN, split_axis=2, concat_axis=1, tiled=True)  14.5 us
    all_gather x1, waiting for transfers between devices, rows_first(): result, at, done = (lax.all_gather(both, axis, axis=0, tiled=True), 0, [])  12.1 us
    all_gather x1, blocking collectives, whole_of(): shard = lax.all_gather(shard, axis, axis=dim, tiled=True)  10.6 us
    all_to_all x1, starting transfers between devices, from_everyone(): lax.all_to_all(jnp.broadcast_to(shard[None], (devices, *shard.shape)), ax...  10.5 us
    ppermute x1, starting transfers between devices, extended_2(): lax.ppermute(tail, axis, [(i, (i + 1) % count) for i in range(ends)])  7.37 us
    dot_general x9, matrix products, conv_taps(): jnp.einsum('oc,ncrw->norw', taps_weight[row_tap, col_tap], window, prefer...  7.3 us
  transfers between devices with their start and end apart: 7, of which 6 were waited for; matrix products, arithmetic and copies ran while one was open for 9% of the time, Pallas kernels for 0%

commit v1 on v0

v1 whole, which is shorter than its diff:
```python
import functools

import jax
import jax.numpy as jnp
from jax import lax
from jax.experimental import pallas as pl
from jax.experimental.pallas import tpu as pltpu
from jax.sharding import Mesh
from jax.sharding import PartitionSpec as P

D = 256
GROUPS = 32
IN_CH = 192
COLS = 512
QUERIES = 200
BAND = ("band_0", "band_1", "band_2")
CHAN = ("chan_0", "chan_1")
ALL = BAND + CHAN
EPS = 1e-05
F32 = jnp.float32
BF16 = jnp.bfloat16
FINE_ROWS = 96
COARSE_AT = 96
CONV_AT = 192
MASK_AT = 264
VEC_AT = 280
BULK_ROWS = 288


def dot(a, b):
    return lax.dot_general(a, b, (((1,), (0,)), ((), ())), preferred_element_type=F32)


def local_stats(values, lane, offset):
    blocks = values.reshape(GROUPS, D // GROUPS, COLS)
    count = D // GROUPS * COLS
    mean = jnp.sum(jnp.sum(blocks, axis=2, keepdims=True), axis=1, keepdims=True) / count
    dev = blocks - mean
    m2 = jnp.sum(jnp.sum(dev * dev, axis=2, keepdims=True), axis=1, keepdims=True)
    group = lax.broadcasted_iota(jnp.int32, (GROUPS, 1, 128), 0)
    row = jnp.where(lane == group + offset, mean, 0.0)
    row = row + jnp.where(lane == group + (offset + GROUPS), m2, 0.0)
    return jnp.sum(row, axis=0)


def combined_stats(stats, image):
    devices = stats.shape[0]
    count = D // GROUPS * COLS
    mean = jnp.sum(stats, axis=0, keepdims=True) / devices
    dev = stats - mean
    spread = jnp.sum(dev * dev, axis=0, keepdims=True) * (1.0 / devices)
    inner = mean * (1.0 / count)
    lane = lax.broadcasted_iota(jnp.int32, (D, 128), 1)
    group = lax.broadcasted_iota(jnp.int32, (D, 128), 0) // (D // GROUPS)
    at_mean = lane == group + image * 2 * GROUPS
    at_m2 = lane == group + (image * 2 + 1) * GROUPS
    mean_col = jnp.sum(jnp.where(at_mean, mean, 0.0), axis=1, keepdims=True)
    var_col = jnp.sum(
        jnp.where(at_mean, spread, 0.0) + jnp.where(at_m2, inner, 0.0), axis=1, keepdims=True
    )
    return mean_col, var_col


def vector_col(bulk_ref, index):
    lane = lax.broadcasted_iota(jnp.int32, (32, 128), 1)
    row = lax.broadcasted_iota(jnp.int32, (32, 128), 0)
    pieces = []
    for s in range(8):
        vec = bulk_ref[s, VEC_AT : VEC_AT + 8, 0:128].astype(F32)[index : index + 1, :]
        pieces.append(jnp.sum(jnp.where(lane == row, vec, 0.0), axis=1, keepdims=True))
    return jnp.concatenate(pieces, axis=0)


def fine_row(ref, at):
    return jnp.concatenate([ref[s, at : at + 24, :] for s in range(8)], axis=0)


def lateral_kernel(own_ref, weight_ref, stats_ref):
    for s in range(8):
        for half in range(2):
            weight_ref[32 * s + 16 * half : 32 * s + 16 * half + 16, :] = own_ref[
                s, 48:64, 256 * half : 256 * half + 256
            ]
    lane = lax.broadcasted_iota(jnp.int32, (GROUPS, 1, 128), 2)
    total = jnp.zeros((1, 128), F32)
    for n in range(2):
        lateral = dot(weight_ref[:, 0:IN_CH], fine_row(own_ref, 24 * n))
        total = total + local_stats(lateral, lane, 64 * n)
    stats_ref[...] = jnp.broadcast_to(total[None], stats_ref.shape)


def conv_kernel(
    own_ref, bulk_ref, other_ref, lat_weight_ref, lat_stats_ref, out_ref, stats_ref,
    weight, joined, up, taps,
):
    core = lax.axis_index("band_2")
    band = (lax.axis_index("band_0") * 2 + lax.axis_index("band_1")) * 2 + core
    parity = lax.axis_index("chan_1")
    chan = lax.axis_index("chan_0") * 2 + parity
    row_at = band * 8 + chan
    for part, ref, base in ((core, bulk_ref, CONV_AT), (1 - core, other_ref, 0)):
        for s in range(8):
            at = pl.multiple_of(32 * s + 16 * part, 16)
            for a in range(3):
                for b in range(3):
                    rows = ref[s, base + (a * 3 + b) * 8 : base + (a * 3 + b) * 8 + 8, :]
                    both = jnp.concatenate([rows[:, 0:256], rows[:, 256:512]], axis=0)
                    weight[b, pl.ds(at, 16), 256 * a : 256 * a + 256] = both
    source = lax.broadcasted_iota(jnp.int32, (256, COLS), 0)
    column = lax.broadcasted_iota(jnp.int32, (256, COLS), 1)
    near = column // 2
    far = jnp.clip(near - 1 + 2 * (column % 2), 0, 255)
    spread = (
        jnp.where(source == near, 0.75, 0.0) + jnp.where(source == far, 0.25, 0.0)
    ).astype(BF16)
    gain = vector_col(bulk_ref, 0)
    shift = vector_col(bulk_ref, 1)
    stats = lat_stats_ref[...].reshape(lat_stats_ref.shape[0], 128)
    lane = lax.broadcasted_iota(jnp.int32, (GROUPS, 1, 128), 2)
    lane_at = lax.broadcasted_iota(jnp.int32, (D, COLS), 1)
    total = jnp.zeros((1, 128), F32)
    for n in range(2):
        mean, var = combined_stats(stats, n)
        scale = lax.rsqrt(var + EPS) * gain
        for k in range(3):
            at = COARSE_AT + 32 * k
            coarse = jnp.concatenate(
                [bulk_ref[s, at : at + 32, 256 * n : 256 * n + 256] for s in range(8)], axis=0
            )
            up[k] = dot(coarse, spread)
        for h in range(3):
            if h == 1:
                fine = fine_row(own_ref, 24 * n)
            else:
                fine = fine_row(bulk_ref, 24 * h + 24 * n)
            lateral = dot(lat_weight_ref[:, 0:IN_CH], fine)
            odd = (parity + h + 1) % 2
            first = (parity + h) // 2
            low = jnp.where(odd == 1, 0.75, 0.25).astype(F32)
            upsampled = low * up[first] + (1.0 - low) * up[first + 1]
            value = ((lateral - mean) * scale + shift + upsampled).astype(BF16)
            inside = jnp.logical_and(row_at + h - 1 >= 0, row_at + h - 1 < 256)
            joined[256 * h : 256 * h + 256, :] = jnp.where(inside, value, jnp.zeros_like(value))
        for b in range(3):
            taps[b] = dot(weight[b], joined[...])
        left = jnp.where(lane_at == 0, 0.0, pltpu.roll(taps[0], 1, axis=1))
        right = jnp.where(lane_at == COLS - 1, 0.0, pltpu.roll(taps[2], COLS - 1, axis=1))
        conv_out = taps[1] + left + right
        out_ref[n] = conv_out
        total = total + local_stats(conv_out, lane, 64 * n)
    stats_ref[...] = jnp.broadcast_to(total[None], stats_ref.shape)


def query_kernel(conv_ref, out_stats_ref, bulk_ref, query_ref, out_ref, weight):
    for s in range(8):
        for half in range(2):
            weight[32 * s + 16 * half : 32 * s + 16 * half + 16, :] = bulk_ref[
                s, MASK_AT : MASK_AT + 16, 256 * half : 256 * half + 256
            ]
    gain = vector_col(bulk_ref, 2)
    shift = vector_col(bulk_ref, 3)
    bias = vector_col(bulk_ref, 4)
    stats = out_stats_ref[...].reshape(out_stats_ref.shape[0], 128)
    for n in range(2):
        mean, var = combined_stats(stats, n)
        scale = lax.rsqrt(var + EPS) * gain
        activated = jnp.maximum((conv_ref[n] - mean) * scale + shift, 0.0).astype(BF16)
        features = (dot(weight[...], activated) + bias).astype(BF16)
        logits = dot(query_ref[...], features)
        shifted = logits - jnp.max(logits, axis=0, keepdims=True)
        result = shifted - jnp.log(jnp.sum(jnp.exp(shifted), axis=0, keepdims=True))
        out_ref[n, :, 0, :] = result


def call(kernel, out_shape, scratch=(), flops=0):
    vmem = pl.BlockSpec(memory_space=pltpu.VMEM)
    single = not isinstance(out_shape, (tuple, list))
    return functools.partial(
        lambda *args: pl.pallas_call(
            kernel,
            out_shape=out_shape,
            in_specs=[vmem] * len(args),
            out_specs=vmem if single else [vmem] * len(out_shape),
            scratch_shapes=list(scratch),
            cost_estimate=pl.CostEstimate(flops=flops, bytes_accessed=1 << 20, transcendentals=0),
            compiler_params=pltpu.CompilerParams(vmem_limit_bytes=40 << 20),
        )(*args)
    )


def per_device(
    fine_features,
    coarse_level,
    lat_weight,
    lat_gain,
    lat_shift,
    out_weight,
    out_gain,
    out_shift,
    mask_weight,
    mask_bias,
    queries,
):
    bands = lax.axis_size(BAND)
    everyone = lax.axis_size(ALL)
    band = lax.axis_index(BAND)
    core = lax.axis_index("band_2")
    fine = jnp.moveaxis(fine_features, 2, 0).reshape(8, 48, COLS)
    coarse = coarse_level.transpose(2, 1, 0, 3).reshape(4, 32, COLS)
    up = [(i, i + 1) for i in range(bands - 1)]
    down = [(i + 1, i) for i in range(bands - 1)]
    above = lax.ppermute(jnp.concatenate([fine[7], coarse[3]], 0), BAND, up)
    below = lax.ppermute(jnp.concatenate([fine[0], coarse[0]], 0), BAND, down)

    weight_rows = jnp.pad(lat_weight, ((0, 0), (0, 256 - IN_CH)))
    weight_rows = weight_rows.reshape(2, 16, 256).transpose(1, 0, 2).reshape(16, 512)
    own = jnp.concatenate([fine, jnp.broadcast_to(weight_rows[None], (8, 16, 512))], 1)
    own = lax.all_to_all(own, CHAN, 0, 0, tiled=True)

    coarse_above = jnp.where(band == 0, coarse[0], above[48:])
    coarse_below = jnp.where(band == bands - 1, coarse[3], below[48:])
    fine_all = jnp.concatenate([above[None, :48], fine, below[None, :48]], 0)
    coarse_all = jnp.concatenate([coarse_above[None], coarse, coarse_below[None]], 0)
    conv = out_weight.reshape(9, 2, 2, 8, 256)
    conv = jnp.where(core == 0, conv[:, 0], conv[:, 1])
    conv = conv.transpose(0, 2, 1, 3).reshape(72, 512)
    mask = mask_weight.reshape(2, 16, 256).transpose(1, 0, 2).reshape(16, 512)
    vectors = jnp.stack([lat_gain, lat_shift, out_gain, out_shift, mask_bias])
    vectors = jnp.pad(vectors, ((0, 3), (0, 512 - 32)))
    shared = jnp.concatenate([conv, mask, vectors], 0)
    bulk = jnp.concatenate(
        [
            fine_all[0:8],
            fine_all[2:10],
            jnp.repeat(coarse_all[0:4], 2, axis=0),
            jnp.repeat(coarse_all[1:5], 2, axis=0),
            jnp.repeat(coarse_all[2:6], 2, axis=0),
            jnp.broadcast_to(shared[None], (8, 96, 512)),
        ],
        1,
    )
    bulk = lax.all_to_all(bulk, CHAN, 0, 0, tiled=True)
    other = lax.ppermute(bulk[:, CONV_AT:MASK_AT], "band_2", [(0, 1), (1, 0)])

    stats_shape = jax.ShapeDtypeStruct((everyone, 1, 128), F32)
    full_lat, stats = call(
        lateral_kernel,
        [jax.ShapeDtypeStruct((D, 256), BF16), stats_shape],
        flops=2 * 2 * 256 * 256 * 512,
    )(own)
    stats = lax.all_to_all(stats, ALL, 0, 0, tiled=True)
    conv_out, stats = call(
        conv_kernel,
        [jax.ShapeDtypeStruct((2, D, COLS), F32), stats_shape],
        (
            pltpu.VMEM((3, D, 3 * D), BF16),
            pltpu.VMEM((3 * D, COLS), BF16),
            pltpu.VMEM((3, D, COLS), F32),
            pltpu.VMEM((3, D, COLS), F32),
        ),
        flops=2 * 2 * 256 * 256 * 512 * 16,
    )(own, bulk, other, full_lat, stats)
    stats = lax.all_to_all(stats, ALL, 0, 0, tiled=True)
    return call(
        query_kernel,
        jax.ShapeDtypeStruct((2, QUERIES, 1, COLS), F32),
        (pltpu.VMEM((D, D), BF16),),
        flops=2 * 2 * 256 * 256 * 512 * 2,
    )(conv_out, stats, bulk, queries)


def solution(mesh):
    finer = Mesh(
        mesh.devices.reshape(8, 2, 2, 4, 2), ("band_0", "band_1", "band_2", "chan_0", "chan_1")
    )
    return jax.shard_map(
        per_device,
        mesh=finer,
        in_specs=(
            P(None, CHAN, BAND, None),
            P(None, CHAN, BAND, None),
            P(CHAN, None),
            P(CHAN),
            P(CHAN),
            P(None, None, CHAN, None),
            P(CHAN),
            P(CHAN),
            P(CHAN, None),
            P(CHAN),
            P(),
        ),
        out_specs=P(None, None, BAND + CHAN, None),
        check_vma=False,
    )
```

time: 196 us -> 121 us (0.62)
  blocking collectives: 64.3 us -> 45.1 us
  waiting for transfers between devices: 56.2 us -> 42 us
  between operations: 13.8 us -> 0.3 us
  matrix products: 11.9 us -> 0 us
  starting transfers between devices: 26.5 us -> 16.5 us
  local copies, waits for them, and re-layouts: 17.5 us -> 7.84 us
  Pallas kernels: 0 us -> 6.51 us
    all_gather x2 -> x0, waiting for transfers between devices: 43.8 us -> none  [the longest x1 31.8 us: whole_of(): shard = lax.all_gather(shard, axis, axis=dim, tiled=True)]
    all_to_all x1 -> x2, waiting for transfers between devices: 2.71 us -> 41.9 us  [the longest x1 32.5 us: per_device(): bulk = lax.all_to_all(bulk, CHAN, 0, 0, tiled=True)]
    psum x5 -> x0, blocking collectives: 39.2 us -> none  [over_axes_2(): return functools.reduce(lax.psum, axes, shard)]
    all_to_all x1 -> x2, blocking collectives: 14.5 us -> 45.1 us  [per_device(): stats = lax.all_to_all(stats, ALL, 0, 0, tiled=True)]
    dot_general x11 -> x0, matrix products: 11.9 us -> none  [the longest x9 7.3 us: conv_taps(): jnp.einsum('oc,ncrw->norw', taps_weight[row_tap, col_tap], window, prefer...]
    all_gather x1 -> x0, blocking collectives: 10.6 us -> none  [whole_of(): shard = lax.all_gather(shard, axis, axis=dim, tiled=True)]
    ppermute x4 -> x3, waiting for transfers between devices: 9.58 us -> 0.16 us  [the longest x1 0.16 us: per_device(): above = lax.ppermute(jnp.concatenate([fine[7], coarse[3]], 0), BAND, up)]
    ppermute x4 -> x3, starting transfers between devices: 15.9 us -> 8.12 us  [the longest x1 5.11 us: per_device(): below = lax.ppermute(jnp.concatenate([fine[0], coarse[0]], 0), BAND, down)]
  transfers between devices with their start and end apart: 7 -> 5, of which waited for: 6 -> 3; matrix products, arithmetic and copies ran while one was open for 9% -> 3% of each run, Pallas kernels for 0% -> 0%
where the time goes in v1:
time: 121 us
  blocking collectives  45.1 us (37%)
  waiting for transfers between devices  42 us (35%)
  starting transfers between devices  16.5 us (14%)
  local copies, waits for them, and re-layouts  7.84 us (6%)
  Pallas kernels  6.51 us (5%)
  other arithmetic  2.5 us (2%)
    all_to_all x2, blocking collectives, per_device(): stats = lax.all_to_all(stats, ALL, 0, 0, tiled=True)  45.1 us
    all_to_all x1, waiting for transfers between devices, per_device(): bulk = lax.all_to_all(bulk, CHAN, 0, 0, tiled=True)  32.5 us
    all_to_all x1, waiting for transfers between devices, per_device(): own = lax.all_to_all(own, CHAN, 0, 0, tiled=True)  9.34 us
    pallas_call x3, Pallas kernels, call(): pl.pallas_call(kernel, out_shape=out_shape, in_specs=[vmem] * len(args),...  6.51 us
    ppermute x1, starting transfers between devices, per_device(): below = lax.ppermute(jnp.concatenate([fine[0], coarse[0]], 0), BAND, down)  5.11 us
    all_to_all x1, starting transfers between devices, per_device(): bulk = lax.all_to_all(bulk, CHAN, 0, 0, tiled=True)  4.93 us
    all_to_all x1, starting transfers between devices, per_device(): own = lax.all_to_all(own, CHAN, 0, 0, tiled=True)  3.49 us
    unnamed x24, local copies, waits for them, and re-layouts  3.4 us
  transfers between devices with their start and end apart: 5, of which 3 were waited for; matrix products, arithmetic and copies ran while one was open for 3% of the time, Pallas kernels for 0%

profile of v1, /device:TPU:1, one launch (start us, length us, event | category | flops | bytes accessed | tf_op | source)
XLA Modules:
  0.0 120.8 jit_solution(13893767708857847851)
XLA Ops:
  0.0 0.0 copy-start.2
  0.0 0.0 copy-start.1
  0.0 0.0 copy-start.4
  0.0 0.0 copy-start.5
  0.0 0.0 copy-start.6
  0.0 0.0 copy-start.7
  0.0 0.0 copy-start.8
  0.0 1.2 fusion.7
  1.3 0.1 copy.20
  1.3 1.1 copy.29
  2.5 5.1 %collective-permute-start.1 = (bf16[80,512]{1,0:T(8,128)(2,1)S(1)}, bf16[80,512]{1,0:T(8,128)(2,1)S(1)}, u32[]{:S(2)}, u32[]{:S(2)}) collective-permute-start(bf16[80,512]{1,0:T(8,128)(2,1)S(1)} %pad_maximum_fusion.6), channel_id=1, source_target_pairs={{8,0},{16,8},{24,16},{32,24},{40,32},{48,40},{56,48},{64,56},{72,6... | collective-permute-start | bytes 245768 | tf_op jit(solution)/shard_map/ppermute | solution.py:213
  7.6 0.1 copy.19
  7.7 3.0 %collective-permute-start = (bf16[80,512]{1,0:T(8,128)(2,1)S(1)}, bf16[80,512]{1,0:T(8,128)(2,1)S(1)}, u32[]{:S(2)}, u32[]{:S(2)}) collective-permute-start(bf16[80,512]{1,0:T(8,128)(2,1)S(1)} %pad_maximum_fusion.5), channel_id=1, source_target_pairs={{0,8},{8,16},{16,24},{24,32},{32,40},{40,48},{48,56},{56,64},{64,7... | collective-permute-start | bytes 245768 | tf_op jit(solution)/shard_map/ppermute | solution.py:212
  10.7 1.0 copy.21
  11.8 0.1 reshape.44
  11.9 0.0 copy-done.2
  11.9 0.0 copy-done.1
  11.9 0.0 copy-done.4
  11.9 0.0 copy-done.5
  11.9 0.0 copy-done.6
  11.9 0.0 copy-done.7
  12.0 0.0 copy-done.8
  12.0 0.2 collective-permute-done
  12.2 0.8 fusion.1
  13.0 0.0 collective-permute-done.1
  13.0 0.8 fusion
  13.8 0.7 constant_dynamic-update-slice_fusion.2
  14.6 0.7 constant_dynamic-update-slice_fusion.1
  15.4 0.8 constant_dynamic-update-slice_fusion
  16.1 1.0 broadcast_dynamic-update-slice_fusion
  17.1 0.0 copy-start.3
  17.1 4.9 %all-to-all-start.1 = ((bf16[8,288,512]{2,1,0:T(8,128)(2,1)}), bf16[8,288,512]{2,1,0:T(8,128)(2,1)S(1)}, u32[]{:S(2)}, u32[]{:S(2)}) async-start(bf16[8,288,512]{2,1,0:T(8,128)(2,1)} %broadcast_dynamic-update-slice_fusion), calls=%async_computation.1 | async-start | bytes 4718592 | tf_op jit(solution)/shard_map/all_to_all | solution.py:242
  22.1 0.0 copy-done.3
  22.1 0.8 pad_maximum_fusion
  23.0 32.5 %all-to-all-done.1.bulk_ref = bf16[8,288,512]{2,1,0:T(8,128)(2,1)S(1)} async-done(((bf16[8,288,512]{2,1,0:T(8,128)(2,1)}), bf16[8,288,512]{2,1,0:T(8,128)(2,1)S(1)}, u32[]{:S(2)}, u32[]{:S(2)}) %all-to-all-start.1) | async-done | bytes 2359328 | tf_op jit(solution)/shard_map/all_to_all | solution.py:242
  55.5 3.5 %all-to-all-start = ((bf16[8,64,512]{2,1,0:T(8,128)(2,1)}), bf16[8,64,512]{2,1,0:T(8,128)(2,1)S(1)}, u32[]{:S(2)}, u32[]{:S(2)}) async-start(bf16[8,64,512]{2,1,0:T(8,128)(2,1)} %pad_maximum_fusion), calls=%async_computation | async-start | bytes 1048576 | tf_op jit(solution)/shard_map/all_to_all | solution.py:218
  59.0 0.9 slice.80
  59.9 0.0 collective-permute-start.2
  59.9 9.3 %all-to-all-done.own_ref = bf16[8,64,512]{2,1,0:T(8,128)(2,1)S(1)} async-done(((bf16[8,64,512]{2,1,0:T(8,128)(2,1)}), bf16[8,64,512]{2,1,0:T(8,128)(2,1)S(1)}, u32[]{:S(2)}, u32[]{:S(2)}) %all-to-all-start) | async-done | bytes 524320 | tf_op jit(solution)/shard_map/all_to_all | solution.py:218
  69.2 0.6 shard_map.109
  69.8 26.8 %all_to_all.20.lat_stats_ref = f32[256,1,128]{2,1,0:T(1,128)S(1)} all-to-all(f32[256,1,128]{2,1,0:T(1,128)S(1)} %get-tuple-element.10), channel_id=1, replica_groups=mesh['band_0'=8,'band_1'=2,'band_2'=2,'chan_0'=4,'chan_1'=2] {'band_0','..., dimensions={0} | all-to-all | bytes 262144 | tf_op jit(solution)/shard_map/all_to_all | solution.py:251
  96.6 0.0 collective-permute-done.2.other_ref
  96.6 0.0 copy-start
  96.6 3.6 %shard_map.110 = (f32[2,256,512]{2,1,0:T(8,128)S(1)}, f32[256,1,128]{2,1,0:T(1,128)S(1)}) custom-call(bf16[8,64,512]{2,1,0:T(8,128)(2,1)S(1)} %all-to-all-done.own_ref, bf16[8,288,512]{2,1,0:T(8,128)(2,1)S(1)} %all-to-all-done.1.bulk_ref, bf16[8,72,512]{2,1,0:T(8,128)(2,1)S(1)} %collective-permute-done.2.other_ref, ...), custom_call_target="tpu_custom_call" | custom-call | flops 2147483648 | bytes 1048576 | tf_op jit(solution)/shard_map/pallas_call | solution.py:179
  100.2 18.3 %all_to_all.21.out_stats_ref = f32[256,1,128]{2,1,0:T(1,128)S(1)} all-to-all(f32[256,1,128]{2,1,0:T(1,128)S(1)} %get-tuple-element.12), channel_id=1, replica_groups=mesh['band_0'=8,'band_1'=2,'band_2'=2,'chan_0'=4,'chan_1'=2] {'band_0','..., dimensions={0} | all-to-all | bytes 262144 | tf_op jit(solution)/shard_map/all_to_all | solution.py:263
  118.5 0.0 copy-done
  118.5 2.3 %shard_map.111 = f32[2,200,1,512]{3,2,1,0:T(1,128)} custom-call(f32[2,256,512]{2,1,0:T(8,128)S(1)} %get-tuple-element.11.conv_ref, f32[256,1,128]{2,1,0:T(1,128)S(1)} %all_to_all.21.out_stats_ref, bf16[8,288,512]{2,1,0:T(8,128)(2,1)S(1)} %all-to-all-done.1.bulk_ref, bf16[200,256]{1,0:T(8,128)(2,1)S(1)} %copy-done), custom_call_target="tpu_custom_call" | custom-call | flops 268435456 | bytes 1048576 | tf_op jit(solution)/shard_map/pallas_call | solution.py:179
  (20 shorter events, 0.2 us)
Async XLA Ops:
  0.0 11.9 %copy-start.2 = (bf16[32,256]{1,0:T(8,128)(2,1)S(1)}, bf16[32,256]{1,0:T(8,128)(2,1)}, u32[]{:S(2)}) copy-start(bf16[32,256]{1,0:T(8,128)(2,1)} %param.19) | copy-start | bytes 49156
  0.0 11.9 %copy-start.1 = (bf16[3,3,32,256]{3,2,1,0:T(8,128)(2,1)S(1)}, bf16[3,3,32,256]{3,2,1,0:T(8,128)(2,1)}, u32[]{:S(2)}) copy-start(bf16[3,3,32,256]{3,2,1,0:T(8,128)(2,1)} %param.16) | copy-start | bytes 442372
  0.0 11.9 %copy-start.4 = (bf16[32]{0:T(256)(128)(2,1)S(1)}, bf16[32]{0:T(256)(128)(2,1)}, u32[]{:S(2)}) copy-start(bf16[32]{0:T(256)(128)(2,1)} %param.14) | copy-start | bytes 196
  0.0 11.9 %copy-start.5 = (bf16[32]{0:T(256)(128)(2,1)S(1)}, bf16[32]{0:T(256)(128)(2,1)}, u32[]{:S(2)}) copy-start(bf16[32]{0:T(256)(128)(2,1)} %param.15) | copy-start | bytes 196
  0.0 11.9 %copy-start.6 = (bf16[32]{0:T(256)(128)(2,1)S(1)}, bf16[32]{0:T(256)(128)(2,1)}, u32[]{:S(2)}) copy-start(bf16[32]{0:T(256)(128)(2,1)} %param.17) | copy-start | bytes 196
  0.0 11.9 %copy-start.7 = (bf16[32]{0:T(256)(128)(2,1)S(1)}, bf16[32]{0:T(256)(128)(2,1)}, u32[]{:S(2)}) copy-start(bf16[32]{0:T(256)(128)(2,1)} %param.18) | copy-start | bytes 196
  0.0 11.9 %copy-start.8 = (bf16[32]{0:T(256)(128)(2,1)S(1)}, bf16[32]{0:T(256)(128)(2,1)}, u32[]{:S(2)}) copy-start(bf16[32]{0:T(256)(128)(2,1)} %param.20) | copy-start | bytes 196
  2.5 10.5 %collective-permute-start.1 = (bf16[80,512]{1,0:T(8,128)(2,1)S(1)}, bf16[80,512]{1,0:T(8,128)(2,1)S(1)}, u32[]{:S(2)}, u32[]{:S(2)}) collective-permute-start(bf16[80,512]{1,0:T(8,128)(2,1)S(1)} %pad_maximum_fusion.6), channel_id=1, source_target_pairs={{8,0},{16,8},{24,16},{32,24},{40,32},{48,40},{56,48},{64,56},{72,6... | collective-permute-start | bytes 245768 | tf_op jit(solution)/shard_map/ppermute | solution.py:213
  7.7 4.5 %collective-permute-start = (bf16[80,512]{1,0:T(8,128)(2,1)S(1)}, bf16[80,512]{1,0:T(8,128)(2,1)S(1)}, u32[]{:S(2)}, u32[]{:S(2)}) collective-permute-start(bf16[80,512]{1,0:T(8,128)(2,1)S(1)} %pad_maximum_fusion.5), channel_id=1, source_target_pairs={{0,8},{8,16},{16,24},{24,32},{32,40},{40,48},{48,56},{56,64},{64,7... | collective-permute-start | bytes 245768 | tf_op jit(solution)/shard_map/ppermute | solution.py:212
  17.1 4.9 %copy-start.3 = (bf16[32,192]{1,0:T(8,128)(2,1)S(1)}, bf16[32,192]{1,0:T(8,128)(2,1)}, u32[]{:S(2)}) copy-start(bf16[32,192]{1,0:T(8,128)(2,1)} %param.13) | copy-start | bytes 36868
  17.1 38.4 %all-to-all-start.1 = ((bf16[8,288,512]{2,1,0:T(8,128)(2,1)}), bf16[8,288,512]{2,1,0:T(8,128)(2,1)S(1)}, u32[]{:S(2)}, u32[]{:S(2)}) async-start(bf16[8,288,512]{2,1,0:T(8,128)(2,1)} %broadcast_dynamic-update-slice_fusion), calls=%async_computation.1 | async-start | bytes 4718592 | tf_op jit(solution)/shard_map/all_to_all | solution.py:242
  55.5 13.7 %all-to-all-start = ((bf16[8,64,512]{2,1,0:T(8,128)(2,1)}), bf16[8,64,512]{2,1,0:T(8,128)(2,1)S(1)}, u32[]{:S(2)}, u32[]{:S(2)}) async-start(bf16[8,64,512]{2,1,0:T(8,128)(2,1)} %pad_maximum_fusion), calls=%async_computation | async-start | bytes 1048576 | tf_op jit(solution)/shard_map/all_to_all | solution.py:218
  59.9 36.7 %collective-permute-start.2 = (bf16[8,72,512]{2,1,0:T(8,128)(2,1)}, bf16[8,72,512]{2,1,0:T(8,128)(2,1)S(1)}, u32[]{:S(2)}, u32[]{:S(2)}) collective-permute-start(bf16[8,72,512]{2,1,0:T(8,128)(2,1)} %slice.80), channel_id=1, source_target_pairs={{0,8},{8,0},{1,9},{9,1},{2,10},{10,2},{3,11},{11,3},{4,12},{12,4},... | collective-permute-start | bytes 1769480 | tf_op jit(solution)/shard_map/ppermute | solution.py:243
  96.6 21.9 %copy-start = (bf16[200,256]{1,0:T(8,128)(2,1)S(1)}, bf16[200,256]{1,0:T(8,128)(2,1)}, u32[]{:S(2)}) copy-start(bf16[200,256]{1,0:T(8,128)(2,1)} %query_ref.1) | copy-start | bytes 307204

commit v2 on v1

--- a/solution.py
+++ b/solution.py
@@ -73,6 +73,49 @@
 
 def fine_row(ref, at):
     return jnp.concatenate([ref[s, at : at + 24, :] for s in range(8)], axis=0)
+
+
+def pack_own_kernel(fine_ref, weight_ref, own_ref, rows):
+    for t in range(4):
+        piece = fine_ref[:, :, :, 128 * t : 128 * t + 128].astype(F32)
+        rows[t] = piece.reshape(48 * 8, 128)
+        for d in range(8):
+            row = rows[t, pl.ds(d, 48, stride=8), :]
+            own_ref[d, 0:48, 128 * t : 128 * t + 128] = row.astype(BF16)
+    weight = jnp.concatenate(
+        [weight_ref[...].astype(F32), jnp.zeros((32, 256 - IN_CH), F32)], axis=1
+    )
+    packed = jnp.concatenate([weight[0:16], weight[16:32]], axis=1).astype(BF16)
+    for d in range(8):
+        own_ref[d, 48:64, :] = packed
+
+
+def pack_bulk_kernel(
+    own_ref, above_ref, below_ref, coarse_ref, conv_ref, mask_ref, vec_ref, bulk_ref
+):
+    core = lax.axis_index("band_2")
+    band = (lax.axis_index("band_0") * 2 + lax.axis_index("band_1")) * 2 + core
+    top = jnp.where(band == 0, coarse_ref[0], above_ref[48:80])
+    bottom = jnp.where(band == 31, coarse_ref[3], below_ref[48:80])
+    for d in range(8):
+        bulk_ref[d, 0:48] = own_ref[d - 1, 0:48] if d else above_ref[0:48]
+        bulk_ref[d, 48:96] = own_ref[d + 1, 0:48] if d < 7 else below_ref[0:48]
+        for k in range(3):
+            at = d // 2 - 1 + k
+            row = top if at < 0 else bottom if at > 3 else coarse_ref[at]
+            bulk_ref[d, COARSE_AT + 32 * k : COARSE_AT + 32 * k + 32] = row
+        bulk_ref[d, VEC_AT : VEC_AT + 8] = vec_ref[...]
+    half = pl.multiple_of(16 * core, 16)
+    for a in range(3):
+        for b in range(3):
+            piece = conv_ref[a, b, pl.ds(half, 16), :].astype(F32)
+            piece = jnp.concatenate([piece[0:8], piece[8:16]], axis=1).astype(BF16)
+            at = CONV_AT + 8 * (3 * a + b)
+            for d in range(8):
+                bulk_ref[d, at : at + 8] = piece
+    mask = jnp.concatenate([mask_ref[0:16], mask_ref[16:32]], axis=1)
+    for d in range(8):
+        bulk_ref[d, MASK_AT : MASK_AT + 16] = mask
 
 
 def lateral_kernel(own_ref, weight_ref, stats_ref):
@@ -203,44 +246,25 @@
 ):
     bands = lax.axis_size(BAND)
     everyone = lax.axis_size(ALL)
-    band = lax.axis_index(BAND)
-    core = lax.axis_index("band_2")
-    fine = jnp.moveaxis(fine_features, 2, 0).reshape(8, 48, COLS)
-    coarse = coarse_level.transpose(2, 1, 0, 3).reshape(4, 32, COLS)
     up = [(i, i + 1) for i in range(bands - 1)]
     down = [(i + 1, i) for i in range(bands - 1)]
-    above = lax.ppermute(jnp.concatenate([fine[7], coarse[3]], 0), BAND, up)
-    below = lax.ppermute(jnp.concatenate([fine[0], coarse[0]], 0), BAND, down)
-
-    weight_rows = jnp.pad(lat_weight, ((0, 0), (0, 256 - IN_CH)))
-    weight_rows = weight_rows.reshape(2, 16, 256).transpose(1, 0, 2).reshape(16, 512)
-    own = jnp.concatenate([fine, jnp.broadcast_to(weight_rows[None], (8, 16, 512))], 1)
-    own = lax.all_to_all(own, CHAN, 0, 0, tiled=True)
-
-    coarse_above = jnp.where(band == 0, coarse[0], above[48:])
-    coarse_below = jnp.where(band == bands - 1, coarse[3], below[48:])
-    fine_all = jnp.concatenate([above[None, :48], fine, below[None, :48]], 0)
-    coarse_all = jnp.concatenate([coarse_above[None], coarse, coarse_below[None]], 0)
-    conv = out_weight.reshape(9, 2, 2, 8, 256)
-    conv = jnp.where(core == 0, conv[:, 0], conv[:, 1])
-    conv = conv.transpose(0, 2, 1, 3).reshape(72, 512)
-    mask = mask_weight.reshape(2, 16, 256).transpose(1, 0, 2).reshape(16, 512)
+    own_out = call(
+        pack_own_kernel,
+        jax.ShapeDtypeStruct((8, 64, COLS), BF16),
+        (pltpu.VMEM((4, 48 * 8, 128), F32),),
+    )(fine_features, lat_weight)
+    own = lax.all_to_all(own_out, CHAN, 0, 0, tiled=True)
+
+    coarse = coarse_level.transpose(2, 1, 0, 3).reshape(4, 32, COLS)
+    above = lax.ppermute(jnp.concatenate([own_out[7, :48], coarse[3]], 0), BAND, up)
+    below = lax.ppermute(jnp.concatenate([own_out[0, :48], coarse[0]], 0), BAND, down)
     vectors = jnp.stack([lat_gain, lat_shift, out_gain, out_shift, mask_bias])
     vectors = jnp.pad(vectors, ((0, 3), (0, 512 - 32)))
-    shared = jnp.concatenate([conv, mask, vectors], 0)
-    bulk = jnp.concatenate(
-        [
-            fine_all[0:8],
-            fine_all[2:10],
-            jnp.repeat(coarse_all[0:4], 2, axis=0),
-            jnp.repeat(coarse_all[1:5], 2, axis=0),
-            jnp.repeat(coarse_all[2:6], 2, axis=0),
-            jnp.broadcast_to(shared[None], (8, 96, 512)),
-        ],
-        1,
-    )
-    bulk = lax.all_to_all(bulk, CHAN, 0, 0, tiled=True)
-    other = lax.ppermute(bulk[:, CONV_AT:MASK_AT], "band_2", [(0, 1), (1, 0)])
+    bulk_out = call(pack_bulk_kernel, jax.ShapeDtypeStruct((8, BULK_ROWS, COLS), BF16))(
+        own_out, above, below, coarse, out_weight, mask_weight, vectors
+    )
+    own, bulk_out = lax.optimization_barrier((own, bulk_out))
+    bulk = lax.all_to_all(bulk_out, CHAN, 0, 0, tiled=True)
 
     stats_shape = jax.ShapeDtypeStruct((everyone, 1, 128), F32)
     full_lat, stats = call(
@@ -249,6 +273,8 @@
         flops=2 * 2 * 256 * 256 * 512,
     )(own)
     stats = lax.all_to_all(stats, ALL, 0, 0, tiled=True)
+    stats, bulk = lax.optimization_barrier((stats, bulk))
+    other = lax.ppermute(bulk[:, CONV_AT:MASK_AT], "band_2", [(0, 1), (1, 0)])
     conv_out, stats = call(
         conv_kernel,
         [jax.ShapeDtypeStruct((2, D, COLS), F32), stats_shape],

time: 121 us -> 113 us (0.934)
  waiting for transfers between devices: 42 us -> 6.62 us
  blocking collectives: 45.1 us -> 77.2 us
  local copies, waits for them, and re-layouts: 7.84 us -> 4.11 us
  other arithmetic: 2.5 us -> 0.01 us
  Pallas kernels: 6.51 us -> 8.69 us
  starting transfers between devices: 16.5 us -> 15.2 us
    all_to_all x2 -> x1, waiting for transfers between devices: 41.9 us -> 0.01 us  [per_device(): own = lax.all_to_all(own_out, CHAN, 0, 0, tiled=True)]
    all_to_all x0 -> x1, blocking collectives: none -> 30.8 us  [per_device(): bulk = lax.all_to_all(bulk_out, CHAN, 0, 0, tiled=True)]
    ppermute x2, waiting for transfers between devices: 0.16 us -> 4.99 us  [the longest x1 4.99 us: per_device(): lax.ppermute(jnp.concatenate([own_out[0, :48], coarse[0]], 0), BAND, down)]
    all_to_all x2 -> x1, starting transfers between devices: 8.42 us -> 5.85 us  [per_device(): own = lax.all_to_all(own_out, CHAN, 0, 0, tiled=True)]
    pallas_call x3 -> x5, Pallas kernels: 6.51 us -> 8.69 us  [call(): pl.pallas_call(kernel, out_shape=out_shape, in_specs=[vmem] * len(args),...]
    ppermute x1, starting transfers between devices: 0.01 us -> 2.04 us  [per_device(): other = lax.ppermute(bulk[:, CONV_AT:MASK_AT], 'band_2', [(0, 1), (1, 0)])]
    unnamed x24, local copies, waits for them, and re-layouts: 3.4 us -> 1.76 us
    ppermute x1, waiting for transfers between devices: 0.01 us -> 1.63 us  [per_device(): other = lax.ppermute(bulk[:, CONV_AT:MASK_AT], 'band_2', [(0, 1), (1, 0)])]
  transfers between devices with their start and end apart: 5 -> 4, of which waited for: 3 -> 2; matrix products, arithmetic and copies ran while one was open for 3% -> 2% of each run, Pallas kernels for 0% -> 1%
where the time goes in v2:
time: 113 us; the launch traced here: 112 us
  blocking collectives  77.2 us (68%)
  starting transfers between devices  15.2 us (13%)
  Pallas kernels  8.69 us (8%)
  waiting for transfers between devices  6.62 us (6%)
  local copies, waits for them, and re-layouts  4.11 us (4%)
    all_to_all x2, blocking collectives, per_device(): stats = lax.all_to_all(stats, ALL, 0, 0, tiled=True)  46.4 us
    all_to_all x1, blocking collectives, per_device(): bulk = lax.all_to_all(bulk_out, CHAN, 0, 0, tiled=True)  30.8 us
    pallas_call x5, Pallas kernels, call(): pl.pallas_call(kernel, out_shape=out_shape, in_specs=[vmem] * len(args),...  8.69 us
    all_to_all x1, starting transfers between devices, per_device(): own = lax.all_to_all(own_out, CHAN, 0, 0, tiled=True)  5.85 us
    ppermute x1, starting transfers between devices, per_device(): lax.ppermute(jnp.concatenate([own_out[7, :48], coarse[3]], 0), BAND, up)  5.37 us
    ppermute x1, waiting for transfers between devices, per_device(): lax.ppermute(jnp.concatenate([own_out[0, :48], coarse[0]], 0), BAND, down)  4.99 us
  transfers between devices with their start and end apart: 4, of which 2 were waited for; matrix products, arithmetic and copies ran while one was open for 2% of the time, Pallas kernels for 1%

profile of v2, /device:TPU:1, one launch (start us, length us, event | category | flops | bytes accessed | tf_op | source)
XLA Modules:
  0.0 112.1 jit_solution(15236628044944291951)
XLA Ops:
  0.0 0.0 copy-start
  0.0 1.0 copy-done
  1.0 0.0 copy-start.3
  1.0 0.7 copy-done.3
  1.7 0.0 copy-start.5
  1.7 0.0 copy-start.6
  1.7 0.0 copy-start.7
  1.7 0.0 copy-start.8
  1.7 0.0 copy-start.9
  1.7 0.0 copy-start.10
  1.7 0.0 copy-start.1
  1.8 0.0 copy-start.4
  1.8 1.0 shard_map.109.own_ref
  2.8 5.9 %all-to-all-start = ((bf16[8,64,512]{2,1,0:T(8,128)(2,1)}), bf16[8,64,512]{2,1,0:T(8,128)(2,1)S(1)}, u32[]{:S(2)}, u32[]{:S(2)}) async-start(bf16[8,64,512]{2,1,0:T(8,128)(2,1)} %shard_map.109.own_ref), calls=%async_computation | async-start | bytes 1048576 | tf_op jit(solution)/shard_map/all_to_all | solution.py:256
  8.6 1.1 fusion
  9.7 0.1 copy.12
  9.8 0.8 slice_bitcast_fusion
  10.6 5.4 %collective-permute-start = (bf16[80,512]{1,0:T(8,128)(2,1)S(1)}, bf16[80,512]{1,0:T(8,128)(2,1)S(1)}, u32[]{:S(2)}, u32[]{:S(2)}) collective-permute-start(bf16[80,512]{1,0:T(8,128)(2,1)S(1)} %pad_maximum_fusion), channel_id=1, source_target_pairs={{0,8},{8,16},{16,24},{24,32},{32,40},{40,48},{48,56},{56,64},{64,7... | collective-permute-start | bytes 245768 | tf_op jit(solution)/shard_map/ppermute | solution.py:259
  16.0 0.1 copy.13
  16.1 1.9 %collective-permute-start.1 = (bf16[80,512]{1,0:T(8,128)(2,1)S(1)}, bf16[80,512]{1,0:T(8,128)(2,1)S(1)}, u32[]{:S(2)}, u32[]{:S(2)}) collective-permute-start(bf16[80,512]{1,0:T(8,128)(2,1)S(1)} %pad_maximum_fusion.1), channel_id=1, source_target_pairs={{8,0},{16,8},{24,16},{32,24},{40,32},{48,40},{56,48},{64,56},{72,6... | collective-permute-start | bytes 245768 | tf_op jit(solution)/shard_map/ppermute | solution.py:260
  18.0 0.0 copy-done.5
  18.0 0.1 copy.14
  18.2 0.1 reshape.7.coarse_ref
  18.3 0.0 copy-done.6
  18.3 0.0 copy-done.7
  18.3 0.0 copy-done.8
  18.3 0.0 copy-done.9
  18.3 0.0 copy-done.10
  18.4 0.0 collective-permute-done.above_ref
  18.4 5.0 %collective-permute-done.1.below_ref = bf16[80,512]{1,0:T(8,128)(2,1)S(1)} collective-permute-done((bf16[80,512]{1,0:T(8,128)(2,1)S(1)}, bf16[80,512]{1,0:T(8,128)(2,1)S(1)}, u32[]{:S(2)}, u32[]{:S(2)}) %collective-permute-start.1) | collective-permute-done | bytes 81952 | tf_op jit(solution)/shard_map/ppermute | solution.py:260
  23.4 0.0 copy-done.1
  23.4 0.0 copy-done.4
  23.4 1.2 %shard_map.110 = bf16[8,288,512]{2,1,0:T(8,128)(2,1)S(1)} custom-call(bf16[8,64,512]{2,1,0:T(8,128)(2,1)} %shard_map.109.own_ref, bf16[80,512]{1,0:T(8,128)(2,1)S(1)} %collective-permute-done.above_ref, bf16[80,512]{1,0:T(8,128)(2,1)S(1)} %collective-permute-done.1.below_ref, bf16[4,32,512]{2,1,0:T(8,128)(2,1)S(1)} %reshape.7.coarse_ref, ...), custom_call_target="tpu_custom_call" | custom-call | bytes 1048576 | tf_op jit(solution)/shard_map/pallas_call | solution.py:222
  24.6 0.0 all-to-all-done.own_ref
  24.6 0.6 shard_map.111
  25.2 27.9 %all_to_all.20.lat_stats_ref = f32[256,1,128]{2,1,0:T(1,128)S(1)} all-to-all(f32[256,1,128]{2,1,0:T(1,128)S(1)} %get-tuple-element.14), channel_id=1, replica_groups=mesh['band_0'=8,'band_1'=2,'band_2'=2,'chan_0'=4,'chan_1'=2] {'band_0','..., dimensions={0} | all-to-all | bytes 262144 | tf_op jit(solution)/shard_map/all_to_all | solution.py:275
  53.1 30.8 %all_to_all.21.bulk_ref = bf16[8,288,512]{2,1,0:T(8,128)(2,1)S(1)} all-to-all(bf16[8,288,512]{2,1,0:T(8,128)(2,1)S(1)} %shard_map.110), channel_id=1, replica_groups=mesh['band_0'=8,'band_1'=2,'band_2'=2,'chan_0'=4,'chan_1'=2] {'chan_0','..., dimensions={0} | all-to-all | bytes 4718592 | tf_op jit(solution)/shard_map/all_to_all | solution.py:267
  84.0 2.0 %collective-permute-start.2 = (bf16[8,72,512]{2,1,0:T(8,128)(2,1)S(1)}, bf16[8,72,512]{2,1,0:T(8,128)(2,1)S(1)}, u32[]{:S(2)}, u32[]{:S(2)}) collective-permute-start(bf16[8,72,512]{2,1,0:T(8,128)(2,1)S(1)} %slice.21), channel_id=1, source_target_pairs={{0,8},{8,0},{1,9},{9,1},{2,10},{10,2},{3,11},{11,3},{4,12},{12,4},... | collective-permute-start | bytes 1769480 | tf_op jit(solution)/shard_map/ppermute | solution.py:277
  86.0 1.6 %collective-permute-done.2.other_ref = bf16[8,72,512]{2,1,0:T(8,128)(2,1)S(1)} collective-permute-done((bf16[8,72,512]{2,1,0:T(8,128)(2,1)S(1)}, bf16[8,72,512]{2,1,0:T(8,128)(2,1)S(1)}, u32[]{:S(2)}, u32[]{:S(2)}) %collective-permute-start.2) | collective-permute-done | bytes 589856 | tf_op jit(solution)/shard_map/ppermute | solution.py:277
  87.7 0.0 copy-start.2
  87.7 3.6 %shard_map.112 = (f32[2,256,512]{2,1,0:T(8,128)S(1)}, f32[256,1,128]{2,1,0:T(1,128)S(1)}) custom-call(bf16[8,64,512]{2,1,0:T(8,128)(2,1)S(1)} %all-to-all-done.own_ref, bf16[8,288,512]{2,1,0:T(8,128)(2,1)S(1)} %all_to_all.21.bulk_ref, bf16[8,72,512]{2,1,0:T(8,128)(2,1)S(1)} %collective-permute-done.2.other_ref, ...), custom_call_target="tpu_custom_call" | custom-call | flops 2147483648 | bytes 1048576 | tf_op jit(solution)/shard_map/pallas_call | solution.py:222
  91.3 18.5 %all_to_all.22.out_stats_ref = f32[256,1,128]{2,1,0:T(1,128)S(1)} all-to-all(f32[256,1,128]{2,1,0:T(1,128)S(1)} %get-tuple-element.20), channel_id=1, replica_groups=mesh['band_0'=8,'band_1'=2,'band_2'=2,'chan_0'=4,'chan_1'=2] {'band_0','..., dimensions={0} | all-to-all | bytes 262144 | tf_op jit(solution)/shard_map/all_to_all | solution.py:289
  109.8 0.0 copy-done.2
  109.8 2.3 %shard_map.113 = f32[2,200,1,512]{3,2,1,0:T(1,128)} custom-call(f32[2,256,512]{2,1,0:T(8,128)S(1)} %get-tuple-element.19.conv_ref, f32[256,1,128]{2,1,0:T(1,128)S(1)} %all_to_all.22.out_stats_ref, bf16[8,288,512]{2,1,0:T(8,128)(2,1)S(1)} %all_to_all.21.bulk_ref, bf16[200,256]{1,0:T(8,128)(2,1)S(1)} %copy-done.2), custom_call_target="tpu_custom_call" | custom-call | flops 268435456 | bytes 1048576 | tf_op jit(solution)/shard_map/pallas_call | solution.py:222
  (7 shorter events, 0.1 us)
Async XLA Ops:
  0.0 1.0 copy-start
  1.0 0.7 copy-start.3
  1.7 16.3 %copy-start.5 = (bf16[2,32,4,256]{3,2,1,0:T(4,128)(2,1)S(1)}, bf16[2,32,4,256]{3,2,1,0:T(4,128)(2,1)}, u32[]{:S(2)}) copy-start(bf16[2,32,4,256]{3,2,1,0:T(4,128)(2,1)} %param.12) | copy-start | bytes 393220
  1.7 16.6 %copy-start.6 = (bf16[32]{0:T(256)(128)(2,1)S(1)}, bf16[32]{0:T(256)(128)(2,1)}, u32[]{:S(2)}) copy-start(bf16[32]{0:T(256)(128)(2,1)} %param.14) | copy-start | bytes 196
  1.7 16.6 %copy-start.7 = (bf16[32]{0:T(256)(128)(2,1)S(1)}, bf16[32]{0:T(256)(128)(2,1)}, u32[]{:S(2)}) copy-start(bf16[32]{0:T(256)(128)(2,1)} %param.15) | copy-start | bytes 196
  1.7 16.6 %copy-start.8 = (bf16[32]{0:T(256)(128)(2,1)S(1)}, bf16[32]{0:T(256)(128)(2,1)}, u32[]{:S(2)}) copy-start(bf16[32]{0:T(256)(128)(2,1)} %param.17) | copy-start | bytes 196
  1.7 16.6 %copy-start.9 = (bf16[32]{0:T(256)(128)(2,1)S(1)}, bf16[32]{0:T(256)(128)(2,1)}, u32[]{:S(2)}) copy-start(bf16[32]{0:T(256)(128)(2,1)} %param.18) | copy-start | bytes 196
  1.7 16.6 %copy-start.10 = (bf16[32]{0:T(256)(128)(2,1)S(1)}, bf16[32]{0:T(256)(128)(2,1)}, u32[]{:S(2)}) copy-start(bf16[32]{0:T(256)(128)(2,1)} %param.20) | copy-start | bytes 196
  1.7 21.6 %copy-start.1 = (bf16[3,3,32,256]{3,2,1,0:T(8,128)(2,1)S(1)}, bf16[3,3,32,256]{3,2,1,0:T(8,128)(2,1)}, u32[]{:S(2)}) copy-start(bf16[3,3,32,256]{3,2,1,0:T(8,128)(2,1)} %conv_ref.1) | copy-start | bytes 442372
  1.8 21.6 %copy-start.4 = (bf16[32,256]{1,0:T(8,128)(2,1)S(1)}, bf16[32,256]{1,0:T(8,128)(2,1)}, u32[]{:S(2)}) copy-start(bf16[32,256]{1,0:T(8,128)(2,1)} %mask_ref.1) | copy-start | bytes 49156
  2.8 21.8 %all-to-all-start = ((bf16[8,64,512]{2,1,0:T(8,128)(2,1)}), bf16[8,64,512]{2,1,0:T(8,128)(2,1)S(1)}, u32[]{:S(2)}, u32[]{:S(2)}) async-start(bf16[8,64,512]{2,1,0:T(8,128)(2,1)} %shard_map.109.own_ref), calls=%async_computation | async-start | bytes 1048576 | tf_op jit(solution)/shard_map/all_to_all | solution.py:256
  10.6 7.7 %collective-permute-start = (bf16[80,512]{1,0:T(8,128)(2,1)S(1)}, bf16[80,512]{1,0:T(8,128)(2,1)S(1)}, u32[]{:S(2)}, u32[]{:S(2)}) collective-permute-start(bf16[80,512]{1,0:T(8,128)(2,1)S(1)} %pad_maximum_fusion), channel_id=1, source_target_pairs={{0,8},{8,16},{16,24},{24,32},{32,40},{40,48},{48,56},{56,64},{64,7... | collective-permute-start | bytes 245768 | tf_op jit(solution)/shard_map/ppermute | solution.py:259
  16.1 7.3 %collective-permute-start.1 = (bf16[80,512]{1,0:T(8,128)(2,1)S(1)}, bf16[80,512]{1,0:T(8,128)(2,1)S(1)}, u32[]{:S(2)}, u32[]{:S(2)}) collective-permute-start(bf16[80,512]{1,0:T(8,128)(2,1)S(1)} %pad_maximum_fusion.1), channel_id=1, source_target_pairs={{8,0},{16,8},{24,16},{32,24},{40,32},{48,40},{56,48},{64,56},{72,6... | collective-permute-start | bytes 245768 | tf_op jit(solution)/shard_map/ppermute | solution.py:260
  84.0 3.7 %collective-permute-start.2 = (bf16[8,72,512]{2,1,0:T(8,128)(2,1)S(1)}, bf16[8,72,512]{2,1,0:T(8,128)(2,1)S(1)}, u32[]{:S(2)}, u32[]{:S(2)}) collective-permute-start(bf16[8,72,512]{2,1,0:T(8,128)(2,1)S(1)} %slice.21), channel_id=1, source_target_pairs={{0,8},{8,0},{1,9},{9,1},{2,10},{10,2},{3,11},{11,3},{4,12},{12,4},... | collective-permute-start | bytes 1769480 | tf_op jit(solution)/shard_map/ppermute | solution.py:277
  87.7 22.1 %copy-start.2 = (bf16[200,256]{1,0:T(8,128)(2,1)S(1)}, bf16[200,256]{1,0:T(8,128)(2,1)}, u32[]{:S(2)}) copy-start(bf16[200,256]{1,0:T(8,128)(2,1)} %query_ref.1) | copy-start | bytes 307204
